TPU v7x, 32 devices: a whole 2x2x4 slice. The times are simulated.
32 devices in a mesh: head: 4 (over y, core), seq: 8 (over z, x).
Axes of the slice: x: 2, y: 2, z: 4, core: 2. Of those that a mesh axis runs over, the one named last changes fastest.
Arguments:
- queries: bfloat16 [8192, 4096], P('seq', 'head'), may hold values from -6 to 6
- keys: bfloat16 [8192, 512], P('seq', 'head'), may hold values from -6 to 6
- values: bfloat16 [8192, 512], P('seq', 'head'), may hold values from -6 to 6
- vertical: int32 [32, 8], P('head'), may hold values from 0 to 63, as said below
- slash: int32 [32, 8], P('head'), may hold values from 1 to 28, as said below
Outputs:
- attended: bfloat16 [8192, 4096], P(('seq', 'head'))
Inputs may be any that keep to these rules, and one draw needn't show every extreme that they name: `vertical`: each row names 8 different blocks. Within each group of 8 consecutive rows, the different blocks named that lie in one slab (blocks s * 8 to s * 8 + 7) number at most 4, and exactly 4 in some slab. `slash`: each row names 8 different offsets.
All inputs are finite; a program needn't handle non-finite values.
Results may differ from a plain program's by a relative error of at most 0.0033.
Values may be sent and summed in bfloat16 or wider, within the bound.
A program may use at most 128 MiB of HBM per device.

v0:
```python
import functools
import math

import jax
import jax.numpy as jnp
from jax import lax
from jax.experimental import pallas as pl
from jax.experimental.pallas import tpu as pltpu
from jax.sharding import PartitionSpec as P

BLK = 128
LARGEST_OFFSET = 28
CAP = 4
NEG = -1e30
PIECES = 2
EARLY = 6
VALUE_STRIDE = 3
MESH = pl.DeviceIdType.MESH


def block_weights(q, own, row, index_ref, bias_ref, kt_ref, causal, listed, factor):
    scores = [jnp.where(causal, jnp.dot(q, kt_ref[own], preferred_element_type=jnp.float32), NEG)]
    for n in range(0, listed, 2):
        a, b = index_ref[row + n], index_ref[row + n + 1]
        pair = jnp.dot(
            q, jnp.concatenate([kt_ref[a], kt_ref[b]], axis=1), preferred_element_type=jnp.float32
        )
        scores.append(pair[:, :BLK] + bias_ref[row + n])
        scores.append(pair[:, BLK:] + bias_ref[row + n + 1])
    top = functools.reduce(jnp.maximum, scores)
    top = jnp.max(top, axis=1, keepdims=True) * factor
    total = None
    rounded = []
    for s in scores:
        w = jnp.exp2(s * factor - top)
        total = w if total is None else total + w
        rounded.append(w.astype(jnp.bfloat16))
    return rounded, jnp.sum(total, axis=1, keepdims=True)


def block_mix(own_weights, pair_weights, total, own, row, index_ref, v_ref, listed):
    mixed = jnp.dot(own_weights, v_ref[own], preferred_element_type=jnp.float32)
    for n in range(0, listed, 2):
        a, b = index_ref[row + n], index_ref[row + n + 1]
        mixed += jnp.dot(
            pair_weights(n),
            jnp.concatenate([v_ref[a], v_ref[b]], axis=0),
            preferred_element_type=jnp.float32,
        )
    return (mixed / total).astype(jnp.bfloat16)


def layer_kernel(
    slash_ref,
    vertical_ref,
    queries_ref,
    kt_ref,
    v_ref,
    out_ref,
    index_ref,
    bias_ref,
    rank_ref,
    used_ref,
    found_ref,
    pack_ref,
    q_ref,
    kt_buf,
    v_buf,
    staged,
    early_weights,
    early_total,
    held,
    packed,
    held_sem,
    load_sem,
    chain_send,
    chain_recv,
    cross_send,
    cross_recv,
    out_local,
    out_send,
    out_recv,
    *,
    blocks,
    listed,
    width,
    heads,
    slabs,
    groups,
):
    slab = lax.axis_index("seq")
    group = lax.axis_index("head")
    chain_len = slabs // 2
    place, side = slab // 2, slab % 2
    piece = blocks // PIECES
    bufs = (kt_buf, v_buf)
    has_next = place + 1 < chain_len

    whole_blocks = slabs * blocks
    reach = (LARGEST_OFFSET + blocks - 1) // blocks
    pack_at = reach // 2
    cap_piece = CAP // PIECES

    def part(kv, place_of, side_of, c, far):
        origin = place_of * 2 + side_of
        if far:
            first = pl.multiple_of(whole_blocks + origin * CAP + c * cap_piece, cap_piece)
            return bufs[kv].at[pl.ds(first, cap_piece)]
        first = pl.multiple_of(origin * blocks + c * piece, piece)
        return bufs[kv].at[pl.ds(first, piece)]

    def sent(ref, t, kv, c, far):
        if t == pack_at and far:
            return packed.at[kv, pl.ds(c * cap_piece, cap_piece)]
        return ref

    def chain(t, kv, c):
        ref = part(kv, place - t, side, c, chain_far(t + 1))
        return pltpu.make_async_remote_copy(
            sent(ref, t, kv, c, chain_far(t + 1)), ref, chain_send.at[t, kv, c], chain_recv.at[t, kv, c],
            device_id={"seq": slab + 2}, device_id_type=MESH,
        )

    def chain_in(t, kv, c):
        ref = part(kv, place - t, side, c, chain_far(t))
        return pltpu.make_async_remote_copy(
            ref, ref, chain_send.at[t - 1, kv, c], chain_recv.at[t - 1, kv, c],
            device_id={"seq": slab - 2}, device_id_type=MESH,
        )

    def cross(t, kv, c, sender):
        ref = part(kv, place - t, sender, c, cross_far(t, sender))
        return pltpu.make_async_remote_copy(
            sent(ref, t, kv, c, cross_far(t, sender)), ref, cross_send.at[t, kv, c], cross_recv.at[t, kv, c],
            device_id={"seq": place * 2 + 1 - side}, device_id_type=MESH,
        )

    def chain_far(t):
        return 2 * t > reach

    def cross_far(t, sender):
        return (2 * t - 1 if sender else 2 * t + 1) > reach

    def cross_runs(t, sender, this_side):
        if t == 0 and sender == 1:
            return None
        return (side == this_side) & (place >= t)

    own_first = pl.multiple_of(slab * blocks, blocks)
    loads = [
        pltpu.make_async_copy(src, buf.at[pl.ds(own_first, blocks)], load_sem.at[kv])
        for kv, (src, buf) in enumerate(((kt_ref, kt_buf), (v_ref, v_buf)))
    ]
    loads.append(pltpu.make_async_copy(queries_ref, q_ref, load_sem.at[2]))
    for load in loads:
        load.start()

    barrier = pltpu.get_barrier_semaphore()
    pl.semaphore_signal(
        barrier, 1, device_id={"seq": place * 2 + 1 - side}, device_id_type=MESH
    )
    for d in range(1, groups):
        pl.semaphore_signal(
            barrier, 1, device_id={"head": lax.rem(group + d, groups)}, device_id_type=MESH
        )

    @pl.when(has_next)
    def _():
        pl.semaphore_signal(barrier, 1, device_id={"seq": slab + 2}, device_id_type=MESH)

    @pl.when(place > 0)
    def _():
        pl.semaphore_signal(barrier, 1, device_id={"seq": slab - 2}, device_id_type=MESH)

    pl.semaphore_wait(
        barrier, groups + has_next.astype(jnp.int32) + (place > 0).astype(jnp.int32)
    )
    def start_cross(t, kv, c, packed):
        for sender in range(2):
            runs = cross_runs(t, sender, sender)
            if runs is not None and (t == pack_at and cross_far(t, sender)) == packed:

                @pl.when(runs)
                def _():
                    cross(t, kv, c, sender).start()

    def start_chain(t, kv, c, packed):
        if t < chain_len - 1 and (t == pack_at and chain_far(t + 1)) == packed:

            @pl.when((place >= t) & has_next)
            def _():
                chain(t, kv, c).start()

    def pass_on(t, kv, c):
        if t > 0:

            @pl.when(place >= t)
            def _():
                chain_in(t, kv, c).wait_recv()

        start_chain(t, kv, c, False)
        start_cross(t, kv, c, False)
        if t == pack_at and c == PIECES - 1:

            @pl.when(place >= t)
            def _():
                first = pl.multiple_of(((place - t) * 2 + side) * blocks, blocks)
                move = pltpu.make_async_copy(
                    bufs[kv].at[pl.ds(first, blocks)], held.at[kv], held_sem.at[kv]
                )
                move.start()
                move.wait()
                for k in range(CAP):
                    picked = held[kv, 0].astype(jnp.float32) * pack_ref[k * blocks]
                    for n in range(1, blocks):
                        picked += held[kv, n].astype(jnp.float32) * pack_ref[k * blocks + n]
                    packed[kv, k] = picked.astype(jnp.bfloat16)

            for each in range(PIECES):
                start_chain(t, kv, each, True)
                start_cross(t, kv, each, True)

    def wait_cross(kv):
        for t in range(chain_len):
            for c in range(PIECES):
                for sender in range(2):
                    runs = cross_runs(t, sender, 1 - sender)
                    if runs is not None:

                        @pl.when(runs)
                        def _():
                            cross(t, kv, c, sender).wait_recv()

    base = slab * blocks
    slashes, verticals = slash_ref.shape[1], vertical_ref.shape[1]

    def rank_block(block, rank):
        used = block < 0
        for head in range(heads):
            for n in range(verticals):
                used = used | (vertical_ref[head, n] == block)
        rank = jnp.where(block % blocks == 0, 0, rank)
        rank_ref[block] = rank
        used_ref[block] = used.astype(jnp.int32)
        return rank + used.astype(jnp.int32)

    def place_verticals(head, carry):
        for n in range(verticals):
            block = vertical_ref[head, n]
            far = whole_blocks + (block // blocks) * CAP + rank_ref[block]
            found_ref[head * verticals + n] = jnp.where(
                block >= (slab - reach) * blocks, block, far
            )
        return carry

    def list_blocks(step, carry):
        head, own = step // blocks, base + step % blocks
        reached = [own - slash_ref[head, n] for n in range(slashes)]
        for n, block in enumerate(reached):
            ok = block >= 0
            index_ref[step * listed + n] = jnp.where(ok, block, own)
            bias_ref[step * listed + n] = jnp.where(ok, 0.0, NEG)
        for n in range(verticals):
            block = vertical_ref[head, n]
            ok = block < own
            for other in reached:
                ok = ok & (block != other)
            found = found_ref[head * verticals + n]
            index_ref[step * listed + slashes + n] = jnp.where(ok, found, own)
            bias_ref[step * listed + slashes + n] = jnp.where(ok, 0.0, NEG)
        return carry

    lists = heads * blocks
    loads[0].wait()
    for c in range(PIECES):
        pass_on(0, 0, c)
    lax.fori_loop(0, whole_blocks, rank_block, jnp.int32(0))
    packed_first = jnp.maximum((place - pack_at) * 2 + side, 0) * blocks
    for k in range(CAP):
        for n in range(blocks):
            block = packed_first + n
            hit = (used_ref[block] == 1) & (rank_ref[block] == k)
            pack_ref[k * blocks + n] = jnp.where(hit, 1.0, 0.0)
    for t in range(1, chain_len):
        for c in range(PIECES):
            pass_on(t, 0, c)
        if t == 1:
            lax.fori_loop(0, heads, place_verticals, 0)
            lax.fori_loop(0, lists // 4, list_blocks, 0)
        if t == 2:
            lax.fori_loop(lists // 4, lists // 2, list_blocks, 0)
    loads[1].wait()
    for c in range(PIECES):
        pass_on(0, 1, c)
    lax.fori_loop(lists // 2, lists, list_blocks, 0)
    wait_cross(0)
    loads[2].wait()

    factor = math.log2(math.e) / math.sqrt(width)
    causal = lax.broadcasted_iota(jnp.int32, (BLK, BLK), 0) >= lax.broadcasted_iota(
        jnp.int32, (BLK, BLK), 1
    )
    share = blocks // groups
    share_rows = share * BLK

    def out_columns(group_of, head):
        return pl.ds(pl.multiple_of((group_of * heads + head) * width, width), width)

    def out_copy(head, r):
        owner = lax.rem(group + 1 + r, groups)
        return pltpu.make_async_remote_copy(
            staged.at[head, pl.ds(pl.multiple_of(owner * share_rows, share_rows), share_rows)],
            out_ref.at[:, out_columns(group, head)],
            out_send.at[head, r], out_recv.at[head, r],
            device_id={"head": owner}, device_id_type=MESH,
        )

    def out_in(head, r):
        sender = lax.rem(group + groups - 1 - r, groups)
        return pltpu.make_async_remote_copy(
            staged.at[head, pl.ds(0, share_rows)],
            out_ref.at[:, out_columns(sender, head)],
            out_send.at[head, r], out_recv.at[head, r],
            device_id={"head": sender}, device_id_type=MESH,
        )

    def out_own(head):
        return pltpu.make_async_copy(
            staged.at[head, pl.ds(pl.multiple_of(group * share_rows, share_rows), share_rows)],
            out_ref.at[:, out_columns(group, head)],
            out_local.at[head],
        )

    early = early_weights.shape[0]
    values_due = []
    for t in range(1, chain_len):
        each = [[(t, c)] for c in range(PIECES)]
        values_due += [sum(each, [])] if t == pack_at else each

    def owned_blocks(step):
        head, r = step // groups, step % groups
        owner = lax.rem(group + 1 + r, groups)
        columns = pl.ds(pl.multiple_of(head * width, width), width)
        for u in range(share):
            i = owner * share + u
            rows = pl.ds(pl.multiple_of(i * BLK, BLK), BLK)
            yield head, rows, columns, base + i, (head * blocks + i) * listed

    def send_share(step):
        head, r = step // groups, step % groups

        @pl.when(r < groups - 1)
        def _():
            out_copy(head, r).start()

        @pl.when(r == groups - 1)
        def _():
            out_own(head).start()

    def weigh_early(step, carry):
        for k, due in enumerate(values_due):

            @pl.when(step == min(VALUE_STRIDE * (k + 1), early * groups - 1))
            def _():
                for t, c in due:
                    pass_on(t, 1, c)

        for head, rows, columns, own, row in owned_blocks(step):
            rounded, total = block_weights(
                q_ref[rows, columns], own, row, index_ref, bias_ref, kt_buf, causal, listed, factor
            )
            for n, w in enumerate(rounded):
                early_weights[head, rows, n * BLK : (n + 1) * BLK] = w
            early_total[head, rows, :] = jnp.broadcast_to(total, (BLK, width))
        return carry

    def mix_early(step, carry):
        for head, rows, columns, own, row in owned_blocks(step):
            staged[head, rows, :] = block_mix(
                early_weights[head, rows, :BLK],
                lambda n: early_weights[head, rows, (n + 1) * BLK : (n + 3) * BLK],
                early_total[head, rows, :],
                own, row, index_ref, v_buf, listed,
            )
        send_share(step)
        return carry

    def one_share(step, carry):
        for head, rows, columns, own, row in owned_blocks(step):
            rounded, total = block_weights(
                q_ref[rows, columns], own, row, index_ref, bias_ref, kt_buf, causal, listed, factor
            )
            staged[head, rows, :] = block_mix(
                rounded[0],
                lambda n: jnp.concatenate([rounded[1 + n], rounded[2 + n]], axis=1),
                total,
                own, row, index_ref, v_buf, listed,
            )
        send_share(step)
        return carry

    lax.fori_loop(0, early * groups, weigh_early, 0)
    wait_cross(1)
    lax.fori_loop(0, early * groups, mix_early, 0)
    lax.fori_loop(early * groups, heads * groups, one_share, 0)

    for kv in range(2):
        for t in range(chain_len):
            for c in range(PIECES):
                if t < chain_len - 1:

                    @pl.when((place >= t) & has_next)
                    def _():
                        chain(t, kv, c).wait_send()

                for sender in range(2):
                    runs = cross_runs(t, sender, sender)
                    if runs is not None:

                        @pl.when(runs)
                        def _():
                            cross(t, kv, c, sender).wait_send()

    def finish(head, carry):
        out_own(head).wait()
        for r in range(groups - 1):
            out_copy(head, r).wait_send()
            out_in(head, r).wait_recv()
        return carry

    lax.fori_loop(0, heads, finish, 0)


def shards(queries, keys, values, vertical, slash):
    width = keys.shape[1]
    rows = queries.shape[0]
    blocks = rows // BLK
    heads = vertical.shape[0]
    slabs, groups = lax.axis_size("seq"), lax.axis_size("head")
    kt = jnp.swapaxes(keys.reshape(blocks, BLK, width), 1, 2)
    v = values.reshape(blocks, BLK, width)
    listed = slash.shape[1] + vertical.shape[1]
    early = min(EARLY, heads)
    dma = pltpu.SemaphoreType.DMA
    hops = (slabs // 2, 2, PIECES)
    smem, anywhere = pl.BlockSpec(memory_space=pltpu.SMEM), pl.BlockSpec(memory_space=pl.ANY)
    return pl.pallas_call(
        functools.partial(
            layer_kernel,
            blocks=blocks,
            listed=listed,
            width=width,
            heads=heads,
            slabs=slabs,
            groups=groups,
        ),
        in_specs=[smem, smem, anywhere, anywhere, anywhere],
        out_specs=anywhere,
        out_shape=jax.ShapeDtypeStruct((rows // groups, groups * heads * width), jnp.bfloat16),
        scratch_shapes=[
            pltpu.SMEM((heads * blocks * listed,), jnp.int32),
            pltpu.SMEM((heads * blocks * listed,), jnp.float32),
            pltpu.SMEM((slabs * blocks,), jnp.int32),
            pltpu.SMEM((slabs * blocks,), jnp.int32),
            pltpu.SMEM((vertical.size,), jnp.int32),
            pltpu.SMEM((CAP * blocks,), jnp.float32),
            pltpu.VMEM(queries.shape, jnp.bfloat16),
            pltpu.VMEM((slabs * (blocks + CAP), width, BLK), jnp.bfloat16),
            pltpu.VMEM((slabs * (blocks + CAP), BLK, width), jnp.bfloat16),
            pltpu.VMEM((heads, rows, width), jnp.bfloat16),
            pltpu.VMEM((early, rows, (listed + 1) * BLK), jnp.bfloat16),
            pltpu.VMEM((early, rows, width), jnp.float32),
            pltpu.VMEM((2, blocks, BLK, width), jnp.bfloat16),
            pltpu.VMEM((2, CAP, BLK, width), jnp.bfloat16),
            dma((2,)),
            dma((3,)),
            dma(hops),
            dma(hops),
            dma(hops),
            dma(hops),
            dma((heads,)),
            dma((heads, groups - 1)),
            dma((heads, groups - 1)),
        ],
        compiler_params=pltpu.CompilerParams(
            collective_id=0, has_side_effects=True, vmem_limit_bytes=62 * 1024 * 1024
        ),
    )(slash, vertical, queries, kt, v)


def solution(mesh):
    in_specs = (
        P("seq", "head"),
        P("seq", "head"),
        P("seq", "head"),
        P("head", None),
        P("head", None),
    )
    out_specs = P(("seq", "head"), None)
    return jax.shard_map(shards, mesh=mesh, in_specs=in_specs, out_specs=out_specs, check_vma=False)
```

profile of v0, /device:TPU:25, one launch (start us, length us, event | category | flops | bytes accessed | tf_op | source)
XLA Modules:
  0.0 77.9 jit_solution(10293673023400317371)
XLA Ops:
  0.0 1.8 %copy.6 = bf16[8,128,128]{1,2,0:T(8,128)(2,1)} copy(bf16[8,128,128]{2,1,0:T(8,128)(2,1)} %bitcast.5) | data formatting | bytes 524288 | tf_op jit(solution)/shard_map/reshape | solution.py:440
  1.8 73.0 %shard_map.55 = bf16[256,4096]{1,0:T(8,128)(2,1)} custom-call(s32[8,8]{1,0:T(8,128)} %slash_ref.1, s32[8,8]{1,0:T(8,128)} %vertical_ref.1, bf16[1024,1024]{1,0:T(8,128)(2,1)} %queries_ref.1, bf16[8,128,128]{2,1,0:T(8,128)(2,1)} %bitcast.3, bf16[8,128,128]{2,1,0:T(8,128)(2,1)} %bitcast.4), custom_call_target="tpu_custom_call" | custom-call | tf_op jit(solution)/shard_map/pallas_call | solution.py:447
  74.8 3.1 %copy.8 = bf16[256,4096]{1,0:T(8,128)(2,1)} copy(bf16[256,4096]{1,0:T(8,128)(2,1)} %shard_map.55) | data formatting | bytes 4194304
where the time goes:
time: 78.2 us; the launch traced here: 77.9 us
  Pallas kernels  73 us (93%)
  local copies, waits for them, and re-layouts  4.92 us (6%)
    pallas_call x1, Pallas kernels, shards(): pl.pallas_call(functools.partial(layer_kernel, blocks=blocks, listed=list...  73 us
    unnamed x1, local copies, waits for them, and re-layouts  3.13 us
    reshape x1, local copies, waits for them, and re-layouts, shards(): kt = jnp.swapaxes(keys.reshape(blocks, BLK, width), 1, 2)  1.79 us

commit v1 on v0

--- a/solution.py
+++ b/solution.py
@@ -13,62 +13,54 @@
 CAP = 4
 NEG = -1e30
 PIECES = 2
-EARLY = 6
-VALUE_STRIDE = 3
+VALUE_STRIDE = 2
+MIX_UNROLL = 4
+RING = 8
+VMEM_BYTES = 62 * 1024 * 1024
+SPARE_BYTES = 3 * 1024 * 1024
 MESH = pl.DeviceIdType.MESH
 
 
-def block_weights(q, own, row, index_ref, bias_ref, kt_ref, causal, listed, factor):
-    scores = [jnp.where(causal, jnp.dot(q, kt_ref[own], preferred_element_type=jnp.float32), NEG)]
-    for n in range(0, listed, 2):
-        a, b = index_ref[row + n], index_ref[row + n + 1]
-        pair = jnp.dot(
-            q, jnp.concatenate([kt_ref[a], kt_ref[b]], axis=1), preferred_element_type=jnp.float32
-        )
-        scores.append(pair[:, :BLK] + bias_ref[row + n])
-        scores.append(pair[:, BLK:] + bias_ref[row + n + 1])
-    top = functools.reduce(jnp.maximum, scores)
-    top = jnp.max(top, axis=1, keepdims=True) * factor
-    total = None
-    rounded = []
-    for s in scores:
-        w = jnp.exp2(s * factor - top)
-        total = w if total is None else total + w
-        rounded.append(w.astype(jnp.bfloat16))
-    return rounded, jnp.sum(total, axis=1, keepdims=True)
-
-
-def block_mix(own_weights, pair_weights, total, own, row, index_ref, v_ref, listed):
-    mixed = jnp.dot(own_weights, v_ref[own], preferred_element_type=jnp.float32)
-    for n in range(0, listed, 2):
-        a, b = index_ref[row + n], index_ref[row + n + 1]
-        mixed += jnp.dot(
-            pair_weights(n),
-            jnp.concatenate([v_ref[a], v_ref[b]], axis=0),
-            preferred_element_type=jnp.float32,
-        )
-    return (mixed / total).astype(jnp.bfloat16)
+def half_columns(half):
+    return slice(half * BLK, (half + 1) * BLK)
+
+
+def beside(a, b):
+    return jnp.concatenate([a, b], axis=1)
+
+
+def stacked(a, b):
+    return jnp.concatenate([a, b], axis=0)
+
+
+def on_diagonal(a, b):
+    zero = jnp.zeros((BLK, BLK), jnp.bfloat16)
+    return stacked(beside(a, zero), beside(zero, b))
 
 
 def layer_kernel(
     slash_ref,
     vertical_ref,
     queries_ref,
-    kt_ref,
-    v_ref,
+    keys_ref,
+    values_ref,
     out_ref,
     index_ref,
-    bias_ref,
+    slash_bias,
+    vertical_bias,
     rank_ref,
     used_ref,
     found_ref,
     pack_ref,
     q_ref,
-    kt_buf,
+    k_buf,
     v_buf,
     staged,
-    early_weights,
-    early_total,
+    weights,
+    scores_even,
+    scores_odd,
+    top_even,
+    top_odd,
     held,
     packed,
     held_sem,
@@ -82,7 +74,7 @@
     out_recv,
     *,
     blocks,
-    listed,
+    rounds,
     width,
     heads,
     slabs,
@@ -93,7 +85,7 @@
     chain_len = slabs // 2
     place, side = slab // 2, slab % 2
     piece = blocks // PIECES
-    bufs = (kt_buf, v_buf)
+    bufs = (k_buf, v_buf)
     has_next = place + 1 < chain_len
 
     whole_blocks = slabs * blocks
@@ -148,10 +140,10 @@
 
     own_first = pl.multiple_of(slab * blocks, blocks)
     loads = [
-        pltpu.make_async_copy(src, buf.at[pl.ds(own_first, blocks)], load_sem.at[kv])
-        for kv, (src, buf) in enumerate(((kt_ref, kt_buf), (v_ref, v_buf)))
+        pltpu.make_async_copy(keys_ref, k_buf.at[pl.ds(own_first, blocks)], load_sem.at[0]),
+        pltpu.make_async_copy(values_ref, held.at[1], load_sem.at[1]),
+        pltpu.make_async_copy(queries_ref, q_ref, load_sem.at[2]),
     ]
-    loads.append(pltpu.make_async_copy(queries_ref, q_ref, load_sem.at[2]))
     for load in loads:
         load.start()
 
@@ -211,10 +203,7 @@
                 move.start()
                 move.wait()
                 for k in range(CAP):
-                    picked = held[kv, 0].astype(jnp.float32) * pack_ref[k * blocks]
-                    for n in range(1, blocks):
-                        picked += held[kv, n].astype(jnp.float32) * pack_ref[k * blocks + n]
-                    packed[kv, k] = picked.astype(jnp.bfloat16)
+                    packed[kv, k] = held[kv, pack_ref[k]]
 
             for each in range(PIECES):
                 start_chain(t, kv, each, True)
@@ -248,9 +237,8 @@
         for n in range(verticals):
             block = vertical_ref[head, n]
             far = whole_blocks + (block // blocks) * CAP + rank_ref[block]
-            found_ref[head * verticals + n] = jnp.where(
-                block >= (slab - reach) * blocks, block, far
-            )
+            found = jnp.where(block >= (slab - reach) * blocks, block, far)
+            found_ref[head * verticals + n] = jnp.where(block < base + blocks, found, base)
         return carry
 
     def list_blocks(step, carry):
@@ -258,16 +246,14 @@
         reached = [own - slash_ref[head, n] for n in range(slashes)]
         for n, block in enumerate(reached):
             ok = block >= 0
-            index_ref[step * listed + n] = jnp.where(ok, block, own)
-            bias_ref[step * listed + n] = jnp.where(ok, 0.0, NEG)
+            index_ref[step * slashes + n] = jnp.where(ok, block, own)
+            slash_bias[step * slashes + n] = jnp.where(ok, 0.0, NEG)
         for n in range(verticals):
             block = vertical_ref[head, n]
             ok = block < own
             for other in reached:
                 ok = ok & (block != other)
-            found = found_ref[head * verticals + n]
-            index_ref[step * listed + slashes + n] = jnp.where(ok, found, own)
-            bias_ref[step * listed + slashes + n] = jnp.where(ok, 0.0, NEG)
+            vertical_bias[step * verticals + n] = jnp.where(ok, 0.0, NEG)
         return carry
 
     lists = heads * blocks
@@ -277,10 +263,15 @@
     lax.fori_loop(0, whole_blocks, rank_block, jnp.int32(0))
     packed_first = jnp.maximum((place - pack_at) * 2 + side, 0) * blocks
     for k in range(CAP):
+        at = jnp.int32(0)
         for n in range(blocks):
             block = packed_first + n
             hit = (used_ref[block] == 1) & (rank_ref[block] == k)
-            pack_ref[k * blocks + n] = jnp.where(hit, 1.0, 0.0)
+            at = at + jnp.where(hit, n, 0)
+        pack_ref[k] = at
+    loads[1].wait()
+    for n in range(blocks):
+        v_buf[own_first + n] = held[1, n].T
     for t in range(1, chain_len):
         for c in range(PIECES):
             pass_on(t, 0, c)
@@ -289,7 +280,6 @@
             lax.fori_loop(0, lists // 4, list_blocks, 0)
         if t == 2:
             lax.fori_loop(lists // 4, lists // 2, list_blocks, 0)
-    loads[1].wait()
     for c in range(PIECES):
         pass_on(0, 1, c)
     lax.fori_loop(lists // 2, lists, list_blocks, 0)
@@ -297,7 +287,7 @@
     loads[2].wait()
 
     factor = math.log2(math.e) / math.sqrt(width)
-    causal = lax.broadcasted_iota(jnp.int32, (BLK, BLK), 0) >= lax.broadcasted_iota(
+    causal = lax.broadcasted_iota(jnp.int32, (BLK, BLK), 0) <= lax.broadcasted_iota(
         jnp.int32, (BLK, BLK), 1
     )
     share = blocks // groups
@@ -306,8 +296,14 @@
     def out_columns(group_of, head):
         return pl.ds(pl.multiple_of((group_of * heads + head) * width, width), width)
 
+    def owner_of(r):
+        return (group // 2 + r // 2 + 1) % (groups // 2) * 2 + (group + r + 1) % 2
+
+    def sender_of(r):
+        return (group // 2 + groups // 2 - 1 - r // 2) % (groups // 2) * 2 + (group + r + 1) % 2
+
     def out_copy(head, r):
-        owner = lax.rem(group + 1 + r, groups)
+        owner = owner_of(r)
         return pltpu.make_async_remote_copy(
             staged.at[head, pl.ds(pl.multiple_of(owner * share_rows, share_rows), share_rows)],
             out_ref.at[:, out_columns(group, head)],
@@ -316,7 +312,7 @@
         )
 
     def out_in(head, r):
-        sender = lax.rem(group + groups - 1 - r, groups)
+        sender = sender_of(r)
         return pltpu.make_async_remote_copy(
             staged.at[head, pl.ds(0, share_rows)],
             out_ref.at[:, out_columns(sender, head)],
@@ -331,78 +327,227 @@
             out_local.at[head],
         )
 
-    early = early_weights.shape[0]
+    listed = 1 + slashes + verticals
+    pairs = heads * blocks // 2 // rounds
+    pairs_of_share = share // 2
+    chunk_count = slashes // 2 + 1
+    live = slab >= 0
     values_due = []
     for t in range(1, chain_len):
         each = [[(t, c)] for c in range(PIECES)]
         values_due += [sum(each, [])] if t == pack_at else each
 
-    def owned_blocks(step):
-        head, r = step // groups, step % groups
-        owner = lax.rem(group + 1 + r, groups)
-        columns = pl.ds(pl.multiple_of(head * width, width), width)
-        for u in range(share):
-            i = owner * share + u
-            rows = pl.ds(pl.multiple_of(i * BLK, BLK), BLK)
-            yield head, rows, columns, base + i, (head * blocks + i) * listed
-
-    def send_share(step):
-        head, r = step // groups, step % groups
-
-        @pl.when(r < groups - 1)
-        def _():
-            out_copy(head, r).start()
-
-        @pl.when(r == groups - 1)
-        def _():
-            out_own(head).start()
-
-    def weigh_early(step, carry):
-        for k, due in enumerate(values_due):
-
-            @pl.when(step == min(VALUE_STRIDE * (k + 1), early * groups - 1))
-            def _():
-                for t, c in due:
-                    pass_on(t, 1, c)
-
-        for head, rows, columns, own, row in owned_blocks(step):
-            rounded, total = block_weights(
-                q_ref[rows, columns], own, row, index_ref, bias_ref, kt_buf, causal, listed, factor
+    def pair_of(pair):
+        r, rest = pair // (heads * pairs_of_share), pair % (heads * pairs_of_share)
+        return r, rest // pairs_of_share, owner_of(r) * share + rest % pairs_of_share * 2
+
+    def listed_pair(buf, pair, n):
+        r, head, i = pair_of(pair)
+        if n == 0:
+            return buf[base + i], buf[base + i + 1]
+        if n <= slashes:
+            row = (head * blocks + i) * slashes + n - 1
+            return buf[index_ref[row]], buf[index_ref[row + slashes]]
+        shared = buf[found_ref[head * verticals + n - 1 - slashes]]
+        return shared, shared
+
+    def bias_of(pair, n, half):
+        r, head, i = pair_of(pair)
+        step = head * blocks + i + half
+        if n <= slashes:
+            return slash_bias[step * slashes + n - 1]
+        return vertical_bias[step * verticals + n - 1 - slashes]
+
+    chunks = []
+    for c in range(chunk_count):
+        near = [0] if c == 0 else [2 * c - 1, 2 * c]
+        chunks.append((near, [1 + slashes + n for n in range(2 * c, min(2 * c + 2, verticals))]))
+
+    def weigh_round(first, *accs):
+        ring = (accs[:RING], accs[RING:])
+        buffers = ((scores_even, top_even), (scores_odd, top_odd))
+
+        def members(c):
+            for j in range(2):
+                for m in range(2):
+                    if j < len(chunks[c][m]):
+                        slot = 2 * c + j if m else max(2 * c - 1, 0) + j
+                        yield m, chunks[c][m][j], ring[m][slot if slot < RING else 1]
+
+        def stage(pair):
+            r, head, i = pair_of(first + pair)
+            columns = pl.ds(pl.multiple_of(head * width, width), width)
+            both = [
+                q_ref[pl.ds(pl.multiple_of((i + u) * BLK, BLK), BLK), columns] for u in range(2)
+            ]
+            pltpu.matmul_push_rhs(on_diagonal(*both), 0, 0, transpose=True)
+            scaled = []
+            for q in both:
+                exact = q.astype(jnp.float32) * factor
+                high = exact.astype(jnp.bfloat16)
+                scaled.append(beside(high, (exact - high.astype(jnp.float32)).astype(jnp.bfloat16)))
+            pltpu.matmul_push_rhs(stacked(*scaled), 0, 1, transpose=True)
+
+        def score(pair, c):
+            fresh = [c == 0, c == 0]
+            for m, n, acc in members(c):
+                pltpu.matmul_acc_lhs(
+                    acc, beside(*listed_pair(k_buf, first + pair, n)), load_staged_rhs=0 if fresh[m] else None
+                )
+                fresh[m] = False
+
+        def take(pair, c, scores, top):
+            tops = [None, None]
+            for m, n, acc in members(c):
+                both = pltpu.matmul_pop(acc)
+                for half in range(2):
+                    x = both[:, half_columns(half)]
+                    if n == 0:
+                        x = jnp.where(causal, x, NEG)
+                    scores[n * BLK : (n + 1) * BLK, half_columns(half)] = x
+                    x = jnp.max(x.reshape(BLK // 8, 8, BLK), axis=0)
+                    if n > 0:
+                        x = x + bias_of(first + pair, n, half)
+                    if m == 0:
+                        x = x * factor
+                    tops[half] = x if tops[half] is None else jnp.maximum(tops[half], x)
+            for half in range(2):
+                x = tops[half]
+                if c > 0:
+                    x = jnp.maximum(x, top[:, half_columns(half)])
+                if c == chunk_count - 1:
+                    x = jnp.broadcast_to(jnp.max(x, axis=0, keepdims=True), (8, BLK))
+                top[:, half_columns(half)] = x
+
+        def weigh(pair, c, scores, top):
+            for m, n, _ in members(c):
+                for half in range(2):
+                    x = scores[n * BLK : (n + 1) * BLK, half_columns(half)]
+                    shift = top[0:1, half_columns(half)]
+                    if n > 0:
+                        shift = shift - bias_of(first + pair, n, half)
+                    if m == 0:
+                        x = x * factor
+                    weights[pair, n * BLK : (n + 1) * BLK, half_columns(half)] = jnp.exp2(
+                        x - shift
+                    ).astype(jnp.bfloat16)
+
+        def one_pair(step, parity):
+            now = step
+            last, older = jnp.maximum(step - 1, 0), jnp.maximum(step - 2, 0)
+            mine, other = buffers[parity], buffers[1 - parity]
+
+            def part(c):
+                if c == 0:
+                    score(now, 0)
+                    take(last, chunk_count - 2, *other)
+                    weigh(older, chunk_count - 2, *mine)
+                elif c == 1:
+                    take(last, chunk_count - 1, *other)
+                    score(now, 1)
+                    weigh(older, chunk_count - 1, *mine)
+                else:
+                    score(now, c)
+                    if c == chunk_count - 1:
+                        stage(jnp.minimum(step + 1, pairs - 1))
+                    take(now, c - 2, *mine)
+                    weigh(last, c - 2, *other)
+
+            for c in range(chunk_count):
+                pl.when(live)(functools.partial(part, c))
+
+        for m in range(2):
+            for acc in ring[m]:
+                pltpu.matmul_pop(acc)
+        stage(0)
+
+        def two_pairs(step, carry):
+            if first == 0:
+                for k, due in enumerate(values_due):
+
+                    @pl.when(step == min(VALUE_STRIDE * (k + 1), pairs // 2 - 1))
+                    def _():
+                        for t, c in due:
+                            pass_on(t, 1, c)
+
+            one_pair(2 * step, 0)
+            one_pair(2 * step + 1, 1)
+            return carry
+
+        lax.fori_loop(0, pairs // 2, two_pairs, 0)
+        for c in range(chunk_count - 2, chunk_count):
+            take(pairs - 1, c, *buffers[1])
+            weigh(pairs - 2, c, *buffers[0])
+        for c in range(chunk_count):
+            weigh(pairs - 1, c, *buffers[1])
+        for m in range(2):
+            pltpu.matmul_acc_lhs(
+                ring[m][0], jnp.zeros((BLK, 2 * BLK), jnp.bfloat16), load_staged_rhs=0
             )
-            for n, w in enumerate(rounded):
-                early_weights[head, rows, n * BLK : (n + 1) * BLK] = w
-            early_total[head, rows, :] = jnp.broadcast_to(total, (BLK, width))
-        return carry
-
-    def mix_early(step, carry):
-        for head, rows, columns, own, row in owned_blocks(step):
-            staged[head, rows, :] = block_mix(
-                early_weights[head, rows, :BLK],
-                lambda n: early_weights[head, rows, (n + 1) * BLK : (n + 3) * BLK],
-                early_total[head, rows, :],
-                own, row, index_ref, v_buf, listed,
-            )
-        send_share(step)
-        return carry
-
-    def one_share(step, carry):
-        for head, rows, columns, own, row in owned_blocks(step):
-            rounded, total = block_weights(
-                q_ref[rows, columns], own, row, index_ref, bias_ref, kt_buf, causal, listed, factor
-            )
-            staged[head, rows, :] = block_mix(
-                rounded[0],
-                lambda n: jnp.concatenate([rounded[1 + n], rounded[2 + n]], axis=1),
-                total,
-                own, row, index_ref, v_buf, listed,
-            )
-        send_share(step)
-        return carry
-
-    lax.fori_loop(0, early * groups, weigh_early, 0)
-    wait_cross(1)
-    lax.fori_loop(0, early * groups, mix_early, 0)
-    lax.fori_loop(early * groups, heads * groups, one_share, 0)
+            pltpu.matmul_pop(ring[m][0])
+
+    def mix_round(first, *accs):
+        ones = jnp.ones((16, 2 * BLK), jnp.bfloat16)
+
+        def mix(pair, m, acc):
+            slot = 0
+            for n in range(1 + slashes):
+                w = weights[pair, n * BLK : (n + 1) * BLK, :]
+                pltpu.matmul_push_rhs(on_diagonal(w[:, :BLK], w[:, BLK:]), slot, m)
+                lhs = beside(*listed_pair(v_buf, first + pair, n))
+                pltpu.matmul_acc_lhs(acc, stacked(lhs, ones), load_staged_rhs=slot)
+                slot = 1 - slot
+                yield
+            for n in range(1 + slashes, listed, 2):
+                pltpu.matmul_push_rhs(weights[pair, n * BLK : (n + 2) * BLK, :], slot, m)
+                lhs = beside(*[listed_pair(v_buf, first + pair, n + u)[0] for u in range(2)])
+                pltpu.matmul_acc_lhs(acc, stacked(lhs, ones), load_staged_rhs=slot)
+                slot = 1 - slot
+                yield
+
+        def some_pairs(step, carry):
+            at = step * 2 * MIX_UNROLL
+            for u in range(MIX_UNROLL):
+                for _ in zip(
+                    mix(at + 2 * u, 0, accs[u]), mix(at + 2 * u + 1, 1, accs[MIX_UNROLL + u])
+                ):
+                    pass
+            for u in range(MIX_UNROLL):
+                for m in range(2):
+                    r, head, i = pair_of(first + at + 2 * u + m)
+                    mixed = pltpu.matmul_pop(accs[m * MIX_UNROLL + u])
+                    for half in range(2):
+                        out = mixed[:width, half_columns(half)] / mixed[width : width + 1, half_columns(half)]
+                        rows = pl.ds(pl.multiple_of((i + half) * BLK, BLK), BLK)
+                        staged[head, rows, :] = out.T.astype(jnp.bfloat16)
+            for u in range(2 * MIX_UNROLL // pairs_of_share):
+                r, head, i = pair_of(first + at + u * pairs_of_share)
+
+                @pl.when(r < groups - 1)
+                def _():
+                    out_copy(head, r).start()
+
+                @pl.when(r == groups - 1)
+                def _():
+                    out_own(head).start()
+
+            return carry
+
+        for acc in accs:
+            pltpu.matmul_pop(acc)
+        lax.fori_loop(0, pairs // (2 * MIX_UNROLL), some_pairs, 0)
+
+    for each in range(rounds):
+        pl.run_scoped(
+            functools.partial(weigh_round, each * pairs),
+            *[pltpu.ACC(m)((BLK, 2 * BLK), jnp.float32) for m in range(2) for _ in range(RING)],
+        )
+        if each == 0:
+            wait_cross(1)
+        pl.run_scoped(
+            functools.partial(mix_round, each * pairs),
+            *[pltpu.ACC(m)((width + 16, 2 * BLK), jnp.float32) for m in range(2) for _ in range(MIX_UNROLL)],
+        )
 
     for kv in range(2):
         for t in range(chain_len):
@@ -437,10 +582,16 @@
     blocks = rows // BLK
     heads = vertical.shape[0]
     slabs, groups = lax.axis_size("seq"), lax.axis_size("head")
-    kt = jnp.swapaxes(keys.reshape(blocks, BLK, width), 1, 2)
+    k = keys.reshape(blocks, BLK, width)
     v = values.reshape(blocks, BLK, width)
-    listed = slash.shape[1] + vertical.shape[1]
-    early = min(EARLY, heads)
+    slashes, verticals = slash.shape[1], vertical.shape[1]
+    listed = 1 + slashes + verticals
+    pairs = heads * blocks // 2
+    room = VMEM_BYTES - 4 * (2 * BLK * width * slabs * (blocks + CAP) // 2)
+    room -= 4 * rows * heads * width + 2 * 4 * listed * BLK * 2 * BLK + SPARE_BYTES
+    rounds = 1
+    while pairs // rounds * listed * BLK * 2 * BLK * 2 > room:
+        rounds *= 2
     dma = pltpu.SemaphoreType.DMA
     hops = (slabs // 2, 2, PIECES)
     smem, anywhere = pl.BlockSpec(memory_space=pltpu.SMEM), pl.BlockSpec(memory_space=pl.ANY)
@@ -448,7 +599,7 @@
         functools.partial(
             layer_kernel,
             blocks=blocks,
-            listed=listed,
+            rounds=rounds,
             width=width,
             heads=heads,
             slabs=slabs,
@@ -458,18 +609,22 @@
         out_specs=anywhere,
         out_shape=jax.ShapeDtypeStruct((rows // groups, groups * heads * width), jnp.bfloat16),
         scratch_shapes=[
-            pltpu.SMEM((heads * blocks * listed,), jnp.int32),
-            pltpu.SMEM((heads * blocks * listed,), jnp.float32),
+            pltpu.SMEM((heads * blocks * slashes,), jnp.int32),
+            pltpu.SMEM((heads * blocks * slashes,), jnp.float32),
+            pltpu.SMEM((heads * blocks * verticals,), jnp.float32),
             pltpu.SMEM((slabs * blocks,), jnp.int32),
             pltpu.SMEM((slabs * blocks,), jnp.int32),
             pltpu.SMEM((vertical.size,), jnp.int32),
-            pltpu.SMEM((CAP * blocks,), jnp.float32),
+            pltpu.SMEM((CAP,), jnp.int32),
             pltpu.VMEM(queries.shape, jnp.bfloat16),
+            pltpu.VMEM((slabs * (blocks + CAP), BLK, width), jnp.bfloat16),
             pltpu.VMEM((slabs * (blocks + CAP), width, BLK), jnp.bfloat16),
-            pltpu.VMEM((slabs * (blocks + CAP), BLK, width), jnp.bfloat16),
             pltpu.VMEM((heads, rows, width), jnp.bfloat16),
-            pltpu.VMEM((early, rows, (listed + 1) * BLK), jnp.bfloat16),
-            pltpu.VMEM((early, rows, width), jnp.float32),
+            pltpu.VMEM((pairs // rounds, listed * BLK, 2 * BLK), jnp.bfloat16),
+            pltpu.VMEM((listed * BLK, 2 * BLK), jnp.float32),
+            pltpu.VMEM((listed * BLK, 2 * BLK), jnp.float32),
+            pltpu.VMEM((8, 2 * BLK), jnp.float32),
+            pltpu.VMEM((8, 2 * BLK), jnp.float32),
             pltpu.VMEM((2, blocks, BLK, width), jnp.bfloat16),
             pltpu.VMEM((2, CAP, BLK, width), jnp.bfloat16),
             dma((2,)),
@@ -483,9 +638,9 @@
             dma((heads, groups - 1)),
         ],
         compiler_params=pltpu.CompilerParams(
-            collective_id=0, has_side_effects=True, vmem_limit_bytes=62 * 1024 * 1024
+            collective_id=0, has_side_effects=True, vmem_limit_bytes=VMEM_BYTES
         ),
-    )(slash, vertical, queries, kt, v)
+    )(slash, vertical, queries, k, v)
 
 
 def solution(mesh):

time: 78.2 us -> 76.5 us (0.978)
  the two profiles are of different devices: /device:TPU:25 before, /device:TPU:24 now
where the time goes in v1:
time: 76.5 us; the launch traced here: 76.3 us
  Pallas kernels  73.2 us (96%)
  local copies, waits for them, and re-layouts  3.13 us (4%)
    pallas_call x1, Pallas kernels, shards(): pl.pallas_call(functools.partial(layer_kernel, blocks=blocks, rounds=roun...  73.2 us
    unnamed x1, local copies, waits for them, and re-layouts  3.13 us

profile of v1, /device:TPU:24, one launch (start us, length us, event | category | flops | bytes accessed | tf_op | source)
XLA Modules:
  0.0 76.3 jit_solution(5998286000111011163)
XLA Ops:
  0.0 73.2 %shard_map.55 = bf16[256,4096]{1,0:T(8,128)(2,1)} custom-call(s32[8,8]{1,0:T(8,128)} %slash_ref.1, s32[8,8]{1,0:T(8,128)} %vertical_ref.1, bf16[1024,1024]{1,0:T(8,128)(2,1)} %queries_ref.1, bf16[8,128,128]{2,1,0:T(8,128)(2,1)} %bitcast.2, bf16[8,128,128]{2,1,0:T(8,128)(2,1)} %bitcast.3), custom_call_target="tpu_custom_call" | custom-call | tf_op jit(solution)/shard_map/pallas_call | solution.py:598
  73.2 3.1 %copy.7 = bf16[256,4096]{1,0:T(8,128)(2,1)} copy(bf16[256,4096]{1,0:T(8,128)(2,1)} %shard_map.55) | data formatting | bytes 4194304

commit v2 on v1

--- a/solution.py
+++ b/solution.py
@@ -1,4 +1,5 @@
 import functools
+import itertools
 import math
 
 import jax
@@ -13,8 +14,9 @@
 CAP = 4
 NEG = -1e30
 PIECES = 2
-VALUE_STRIDE = 2
+VALUE_STEPS = (3, 7, 8, 9, 12)
 MIX_UNROLL = 4
+GATED = True
 RING = 8
 VMEM_BYTES = 62 * 1024 * 1024
 SPARE_BYTES = 3 * 1024 * 1024
@@ -45,13 +47,14 @@
     keys_ref,
     values_ref,
     out_ref,
-    index_ref,
-    slash_bias,
-    vertical_bias,
-    rank_ref,
-    used_ref,
+    named_ref,
+    offsets_ref,
     found_ref,
     pack_ref,
+    own_pack_ref,
+    block_ref,
+    bias_even,
+    bias_odd,
     q_ref,
     k_buf,
     v_buf,
@@ -63,6 +66,8 @@
     top_odd,
     held,
     packed,
+    packed_own,
+    turn_sem,
     held_sem,
     load_sem,
     chain_send,
@@ -92,6 +97,8 @@
     reach = (LARGEST_OFFSET + blocks - 1) // blocks
     pack_at = reach // 2
     cap_piece = CAP // PIECES
+    jump = pack_at + 1
+    has_far = place + jump < chain_len
 
     def part(kv, place_of, side_of, c, far):
         origin = place_of * 2 + side_of
@@ -113,6 +120,25 @@
             device_id={"seq": slab + 2}, device_id_type=MESH,
         )
 
+    def direct(kv, c):
+        ref = part(kv, place, side, c, True)
+        return pltpu.make_async_remote_copy(
+            packed_own.at[kv, pl.ds(c * cap_piece, cap_piece)], ref,
+            chain_send.at[pack_at, kv, c], chain_recv.at[pack_at, kv, c],
+            device_id={"seq": slab + 2 * jump}, device_id_type=MESH,
+        )
+
+    def start_direct(kv):
+        for k in range(CAP):
+            block = held[kv, own_pack_ref[k]]
+            packed_own[kv, k] = block.T if kv else block
+
+        for c in range(PIECES):
+
+            @pl.when(has_far)
+            def _():
+                direct(kv, c).start()
+
     def chain_in(t, kv, c):
         ref = part(kv, place - t, side, c, chain_far(t))
         return pltpu.make_async_remote_copy(
@@ -143,6 +169,7 @@
         pltpu.make_async_copy(keys_ref, k_buf.at[pl.ds(own_first, blocks)], load_sem.at[0]),
         pltpu.make_async_copy(values_ref, held.at[1], load_sem.at[1]),
         pltpu.make_async_copy(queries_ref, q_ref, load_sem.at[2]),
+        pltpu.make_async_copy(keys_ref, held.at[0], load_sem.at[3]),
     ]
     for load in loads:
         load.start()
@@ -164,8 +191,25 @@
     def _():
         pl.semaphore_signal(barrier, 1, device_id={"seq": slab - 2}, device_id_type=MESH)
 
+    @pl.when(has_far)
+    def _():
+        pl.semaphore_signal(
+            barrier, 1, device_id={"seq": slab + 2 * jump}, device_id_type=MESH
+        )
+
+    @pl.when(place >= jump)
+    def _():
+        pl.semaphore_signal(
+            barrier, 1, device_id={"seq": slab - 2 * jump}, device_id_type=MESH
+        )
+
     pl.semaphore_wait(
-        barrier, groups + has_next.astype(jnp.int32) + (place > 0).astype(jnp.int32)
+        barrier,
+        groups
+        + has_next.astype(jnp.int32)
+        + (place > 0).astype(jnp.int32)
+        + has_far.astype(jnp.int32)
+        + (place >= jump).astype(jnp.int32),
     )
     def start_cross(t, kv, c, packed):
         for sender in range(2):
@@ -176,38 +220,52 @@
                 def _():
                     cross(t, kv, c, sender).start()
 
-    def start_chain(t, kv, c, packed):
-        if t < chain_len - 1 and (t == pack_at and chain_far(t + 1)) == packed:
-
-            @pl.when((place >= t) & has_next)
+    def chain_runs(t):
+        if t == pack_at:
+            return has_far
+        return (place >= t) & has_next
+
+    def chain_of(t, kv, c):
+        return direct(kv, c) if t == pack_at else chain(t, kv, c)
+
+    def start_chain(t, kv, c):
+        if t < chain_len - 1 and t != pack_at:
+
+            @pl.when(chain_runs(t))
             def _():
                 chain(t, kv, c).start()
 
+    def arrive(t, kv, c):
+        @pl.when(place >= t)
+        def _():
+            chain_in(t, kv, c).wait_recv()
+
+    def pack_arrived(kv):
+        t = pack_at
+
+        @pl.when(place >= t)
+        def _():
+            first = pl.multiple_of(((place - t) * 2 + side) * blocks, blocks)
+            move = pltpu.make_async_copy(
+                bufs[kv].at[pl.ds(first, blocks)], held.at[kv], held_sem.at[kv]
+            )
+            move.start()
+            move.wait()
+            for k in range(CAP):
+                packed[kv, k] = held[kv, pack_ref[k]]
+
+        for each in range(PIECES):
+            start_cross(t, kv, each, True)
+
     def pass_on(t, kv, c):
-        if t > 0:
-
-            @pl.when(place >= t)
-            def _():
-                chain_in(t, kv, c).wait_recv()
-
-        start_chain(t, kv, c, False)
+        arrive(t, kv, c)
+        start_chain(t, kv, c)
         start_cross(t, kv, c, False)
         if t == pack_at and c == PIECES - 1:
-
-            @pl.when(place >= t)
-            def _():
-                first = pl.multiple_of(((place - t) * 2 + side) * blocks, blocks)
-                move = pltpu.make_async_copy(
-                    bufs[kv].at[pl.ds(first, blocks)], held.at[kv], held_sem.at[kv]
-                )
-                move.start()
-                move.wait()
-                for k in range(CAP):
-                    packed[kv, k] = held[kv, pack_ref[k]]
-
-            for each in range(PIECES):
-                start_chain(t, kv, each, True)
-                start_cross(t, kv, each, True)
+            pack_arrived(kv)
+
+    order = [t for t in range(1, chain_len) if t != pack_at]
+    order.insert(min(2, len(order)), pack_at)
 
     def wait_cross(kv):
         for t in range(chain_len):
@@ -223,66 +281,97 @@
     base = slab * blocks
     slashes, verticals = slash_ref.shape[1], vertical_ref.shape[1]
 
-    def rank_block(block, rank):
-        used = block < 0
-        for head in range(heads):
-            for n in range(verticals):
-                used = used | (vertical_ref[head, n] == block)
-        rank = jnp.where(block % blocks == 0, 0, rank)
-        rank_ref[block] = rank
-        used_ref[block] = used.astype(jnp.int32)
-        return rank + used.astype(jnp.int32)
+    low = blocks.bit_length() - 1
+
+    def names(head, words):
+        for n in range(verticals):
+            block = vertical_ref[head, n]
+            bit = jnp.int32(1) << (block & 31)
+            words = tuple(
+                word | jnp.where((block >> 5) == w, bit, 0) for w, word in enumerate(words)
+            )
+        offsets = jnp.int32(0)
+        for n in range(slashes):
+            offsets = offsets | (jnp.int32(1) << slash_ref[head, n])
+        offsets_ref[head] = offsets
+        return words
 
     def place_verticals(head, carry):
         for n in range(verticals):
             block = vertical_ref[head, n]
-            far = whole_blocks + (block // blocks) * CAP + rank_ref[block]
-            found = jnp.where(block >= (slab - reach) * blocks, block, far)
+            first = (block >> low) << low
+            in_slab = named_ref[block >> 5] >> (first & 31)
+            below = in_slab & ((jnp.int32(1) << (block - first)) - 1)
+            rank = jnp.int32(0)
+            for u in range(blocks - 1):
+                rank = rank + ((below >> u) & 1)
+            found = jnp.where(
+                block >= (slab - reach) * blocks, block, whole_blocks + (block >> low) * CAP + rank
+            )
             found_ref[head * verticals + n] = jnp.where(block < base + blocks, found, base)
         return carry
 
-    def list_blocks(step, carry):
-        head, own = step // blocks, base + step % blocks
-        reached = [own - slash_ref[head, n] for n in range(slashes)]
-        for n, block in enumerate(reached):
-            ok = block >= 0
-            index_ref[step * slashes + n] = jnp.where(ok, block, own)
-            slash_bias[step * slashes + n] = jnp.where(ok, 0.0, NEG)
-        for n in range(verticals):
-            block = vertical_ref[head, n]
-            ok = block < own
-            for other in reached:
-                ok = ok & (block != other)
-            vertical_bias[step * verticals + n] = jnp.where(ok, 0.0, NEG)
-        return carry
-
-    lists = heads * blocks
+    def list_pack(to_ref, of_slab):
+        first = of_slab * blocks
+        in_slab = named_ref[first >> 5] >> (first & 31)
+        at = [jnp.int32(0) for _ in range(CAP)]
+        count = jnp.int32(0)
+        for n in range(blocks):
+            hit = (in_slab >> n) & 1
+            at = [x + jnp.where((hit == 1) & (count == k), n, 0) for k, x in enumerate(at)]
+            count = count + hit
+        for k in range(CAP):
+            to_ref[k] = at[k]
+
+    second = group % 2
+    partner = group + 1 - 2 * second
     loads[0].wait()
-    for c in range(PIECES):
-        pass_on(0, 0, c)
-    lax.fori_loop(0, whole_blocks, rank_block, jnp.int32(0))
-    packed_first = jnp.maximum((place - pack_at) * 2 + side, 0) * blocks
-    for k in range(CAP):
-        at = jnp.int32(0)
-        for n in range(blocks):
-            block = packed_first + n
-            hit = (used_ref[block] == 1) & (rank_ref[block] == k)
-            at = at + jnp.where(hit, n, 0)
-        pack_ref[k] = at
+
+    @pl.when(second == 0)
+    def _():
+        for c in range(PIECES):
+            start_chain(0, 0, c)
+            start_cross(0, 0, c, False)
+
+    words = tuple(jnp.int32(0) for _ in range((whole_blocks + 31) // 32))
+    for w, word in enumerate(lax.fori_loop(0, heads, names, words)):
+        named_ref[w] = word
+    list_pack(own_pack_ref, slab)
+    loads[3].wait()
     loads[1].wait()
-    for n in range(blocks):
-        v_buf[own_first + n] = held[1, n].T
-    for t in range(1, chain_len):
+
+    @pl.when(second == 1)
+    def _():
+        if GATED:
+            pl.semaphore_wait(turn_sem, 1)
+        for c in range(PIECES):
+            start_chain(0, 0, c)
+            start_cross(0, 0, c, False)
+
+    start_direct(0)
+    list_pack(pack_ref, jnp.maximum((place - pack_at) * 2 + side, 0))
+    for t in order:
         for c in range(PIECES):
             pass_on(t, 0, c)
         if t == 1:
+            if GATED:
+
+                @pl.when(second == 0)
+                def _():
+                    for sent_t in range(min(2, chain_len - 1)):
+                        for c in range(PIECES):
+
+                            @pl.when(chain_runs(sent_t))
+                            def _():
+                                chain_of(sent_t, 0, c).wait_send()
+
+                    pl.semaphore_signal(
+                        turn_sem, 1, device_id={"head": partner}, device_id_type=MESH
+                    )
+
             lax.fori_loop(0, heads, place_verticals, 0)
-            lax.fori_loop(0, lists // 4, list_blocks, 0)
-        if t == 2:
-            lax.fori_loop(lists // 4, lists // 2, list_blocks, 0)
-    for c in range(PIECES):
-        pass_on(0, 1, c)
-    lax.fori_loop(lists // 2, lists, list_blocks, 0)
+            for n in range(blocks):
+                v_buf[own_first + n] = held[1, n].T
     wait_cross(0)
     loads[2].wait()
 
@@ -331,32 +420,37 @@
     pairs = heads * blocks // 2 // rounds
     pairs_of_share = share // 2
     chunk_count = slashes // 2 + 1
-    live = slab >= 0
-    values_due = []
-    for t in range(1, chain_len):
+    values_due = [[(0, c) for c in range(PIECES)]]
+    for t in order:
         each = [[(t, c)] for c in range(PIECES)]
-        values_due += [sum(each, [])] if t == pack_at else each
+        values_due += [sum(each, [])] if t >= pack_at else each
+
+    for q in range(blocks // 2):
+        block_ref[q] = owner_of(q // pairs_of_share) * share + q % pairs_of_share * 2
 
     def pair_of(pair):
-        r, rest = pair // (heads * pairs_of_share), pair % (heads * pairs_of_share)
-        return r, rest // pairs_of_share, owner_of(r) * share + rest % pairs_of_share * 2
-
-    def listed_pair(buf, pair, n):
-        r, head, i = pair_of(pair)
+        q = lax.div(pair, heads)
+        return lax.rem(pair, heads), q, block_ref[q]
+
+    def reached(head, own, n):
+        return own - slash_ref[head, n - 1]
+
+    def listed_pair(buf, head, i, n):
         if n == 0:
             return buf[base + i], buf[base + i + 1]
         if n <= slashes:
-            row = (head * blocks + i) * slashes + n - 1
-            return buf[index_ref[row]], buf[index_ref[row + slashes]]
+            both = [reached(head, base + i + half, n) for half in range(2)]
+            return [buf[jnp.where(x >= 0, x, base + i + half)] for half, x in enumerate(both)]
         shared = buf[found_ref[head * verticals + n - 1 - slashes]]
         return shared, shared
 
-    def bias_of(pair, n, half):
-        r, head, i = pair_of(pair)
-        step = head * blocks + i + half
+    def bias_of(head, i, n, half):
+        own = base + i + half
         if n <= slashes:
-            return slash_bias[step * slashes + n - 1]
-        return vertical_bias[step * verticals + n - 1 - slashes]
+            return jnp.where(reached(head, own, n) >= 0, 0.0, NEG)
+        back = own - vertical_ref[head, n - 1 - slashes]
+        covered = (offsets_ref[head] >> jnp.clip(back, 0, 31)) & 1
+        return jnp.where((back > 0) & (covered == 0), 0.0, NEG)
 
     chunks = []
     for c in range(chunk_count):
@@ -365,7 +459,9 @@
 
     def weigh_round(first, *accs):
         ring = (accs[:RING], accs[RING:])
-        buffers = ((scores_even, top_even), (scores_odd, top_odd))
+        buffers = (
+            (scores_even, top_even, bias_even), (scores_odd, top_odd, bias_odd)
+        )
 
         def members(c):
             for j in range(2):
@@ -374,8 +470,7 @@
                         slot = 2 * c + j if m else max(2 * c - 1, 0) + j
                         yield m, chunks[c][m][j], ring[m][slot if slot < RING else 1]
 
-        def stage(pair):
-            r, head, i = pair_of(first + pair)
+        def stage(head, i):
             columns = pl.ds(pl.multiple_of(head * width, width), width)
             both = [
                 q_ref[pl.ds(pl.multiple_of((i + u) * BLK, BLK), BLK), columns] for u in range(2)
@@ -388,15 +483,15 @@
                 scaled.append(beside(high, (exact - high.astype(jnp.float32)).astype(jnp.bfloat16)))
             pltpu.matmul_push_rhs(stacked(*scaled), 0, 1, transpose=True)
 
-        def score(pair, c):
+        def score(head, i, c):
             fresh = [c == 0, c == 0]
             for m, n, acc in members(c):
                 pltpu.matmul_acc_lhs(
-                    acc, beside(*listed_pair(k_buf, first + pair, n)), load_staged_rhs=0 if fresh[m] else None
+                    acc, beside(*listed_pair(k_buf, head, i, n)), load_staged_rhs=0 if fresh[m] else None
                 )
                 fresh[m] = False
 
-        def take(pair, c, scores, top):
+        def take(head, i, c, scores, top, biases):
             tops = [None, None]
             for m, n, acc in members(c):
                 both = pltpu.matmul_pop(acc)
@@ -407,10 +502,13 @@
                     scores[n * BLK : (n + 1) * BLK, half_columns(half)] = x
                     x = jnp.max(x.reshape(BLK // 8, 8, BLK), axis=0)
                     if n > 0:
-                        x = x + bias_of(first + pair, n, half)
+                        bias = bias_of(head, i, n, half)
+                        biases[2 * n + half] = bias
+                        x = x + bias
                     if m == 0:
                         x = x * factor
                     tops[half] = x if tops[half] is None else jnp.maximum(tops[half], x)
+                    yield
             for half in range(2):
                 x = tops[half]
                 if c > 0:
@@ -419,67 +517,91 @@
                     x = jnp.broadcast_to(jnp.max(x, axis=0, keepdims=True), (8, BLK))
                 top[:, half_columns(half)] = x
 
-        def weigh(pair, c, scores, top):
+        def weigh(slot, c, scores, top, biases):
             for m, n, _ in members(c):
                 for half in range(2):
                     x = scores[n * BLK : (n + 1) * BLK, half_columns(half)]
                     shift = top[0:1, half_columns(half)]
                     if n > 0:
-                        shift = shift - bias_of(first + pair, n, half)
+                        shift = shift - biases[2 * n + half]
                     if m == 0:
                         x = x * factor
-                    weights[pair, n * BLK : (n + 1) * BLK, half_columns(half)] = jnp.exp2(
+                    weights[slot, half, n * BLK : (n + 1) * BLK, :] = jnp.exp2(
                         x - shift
                     ).astype(jnp.bfloat16)
-
-        def one_pair(step, parity):
-            now = step
+                    yield
+
+        def drain(*steps):
+            for step in steps:
+                for _ in step:
+                    pass
+
+        def alternate(a, b):
+            for _ in itertools.zip_longest(a, b):
+                pass
+
+        def advance(head, q):
+            wraps = head + 1 == heads
+            q = jnp.minimum(q + wraps.astype(jnp.int32), blocks // 2 - 1)
+            return jnp.where(wraps, 0, head + 1), q, block_ref[q]
+
+        def one_pair(step, parity, head, q, i, last_head, last_i):
             last, older = jnp.maximum(step - 1, 0), jnp.maximum(step - 2, 0)
             mine, other = buffers[parity], buffers[1 - parity]
+            next_head, next_q, next_i = advance(head, q)
 
             def part(c):
+                if c == 1:
+                    alternate(
+                        weigh(older, chunk_count - 1, *mine),
+                        take(last_head, last_i, chunk_count - 1, *other),
+                    )
+                    score(head, i, 1)
+                    return
+                score(head, i, c)
                 if c == 0:
-                    score(now, 0)
-                    take(last, chunk_count - 2, *other)
-                    weigh(older, chunk_count - 2, *mine)
-                elif c == 1:
-                    take(last, chunk_count - 1, *other)
-                    score(now, 1)
-                    weigh(older, chunk_count - 1, *mine)
-                else:
-                    score(now, c)
-                    if c == chunk_count - 1:
-                        stage(jnp.minimum(step + 1, pairs - 1))
-                    take(now, c - 2, *mine)
-                    weigh(last, c - 2, *other)
+                    alternate(
+                        weigh(older, chunk_count - 2, *mine),
+                        take(last_head, last_i, chunk_count - 2, *other),
+                    )
+                    return
+                if c == chunk_count - 1:
+                    stage(next_head, next_i)
+                alternate(weigh(last, c - 2, *other), take(head, i, c - 2, *mine))
 
             for c in range(chunk_count):
-                pl.when(live)(functools.partial(part, c))
+                pl.when(slab > -1 - c // 2)(functools.partial(part, c))
+            return next_head, next_q, next_i, head, i
 
         for m in range(2):
             for acc in ring[m]:
                 pltpu.matmul_pop(acc)
-        stage(0)
+        begin = pair_of(jnp.int32(first))
+        stage(begin[0], begin[2])
 
         def two_pairs(step, carry):
             if first == 0:
                 for k, due in enumerate(values_due):
 
-                    @pl.when(step == min(VALUE_STRIDE * (k + 1), pairs // 2 - 1))
+                    @pl.when(step == min(VALUE_STEPS[min(k, len(VALUE_STEPS) - 1)], pairs // 2 - 1))
                     def _():
                         for t, c in due:
-                            pass_on(t, 1, c)
-
-            one_pair(2 * step, 0)
-            one_pair(2 * step + 1, 1)
-            return carry
-
-        lax.fori_loop(0, pairs // 2, two_pairs, 0)
+                            if t == 0:
+                                start_cross(0, 1, c, False)
+                                start_chain(0, 1, c)
+                            else:
+                                pass_on(t, 1, c)
+                        if k == 0:
+                            start_direct(1)
+
+            carry = one_pair(2 * step, 0, *carry)
+            return one_pair(2 * step + 1, 1, *carry)
+
+        carry = lax.fori_loop(0, pairs // 2, two_pairs, (*begin, begin[0], begin[2]))
         for c in range(chunk_count - 2, chunk_count):
-            take(pairs - 1, c, *buffers[1])
-            weigh(pairs - 2, c, *buffers[0])
+            drain(take(*carry[3:], c, *buffers[1]), weigh(pairs - 2, c, *buffers[0]))
         for c in range(chunk_count):
-            weigh(pairs - 1, c, *buffers[1])
+            drain(weigh(pairs - 1, c, *buffers[1]))
         for m in range(2):
             pltpu.matmul_acc_lhs(
                 ring[m][0], jnp.zeros((BLK, 2 * BLK), jnp.bfloat16), load_staged_rhs=0
@@ -490,17 +612,19 @@
         ones = jnp.ones((16, 2 * BLK), jnp.bfloat16)
 
         def mix(pair, m, acc):
+            head, _, i = pair_of(first + pair)
             slot = 0
             for n in range(1 + slashes):
-                w = weights[pair, n * BLK : (n + 1) * BLK, :]
-                pltpu.matmul_push_rhs(on_diagonal(w[:, :BLK], w[:, BLK:]), slot, m)
-                lhs = beside(*listed_pair(v_buf, first + pair, n))
+                both = [weights[pair, half, n * BLK : (n + 1) * BLK, :] for half in range(2)]
+                pltpu.matmul_push_rhs(on_diagonal(*both), slot, m)
+                lhs = beside(*listed_pair(v_buf, head, i, n))
                 pltpu.matmul_acc_lhs(acc, stacked(lhs, ones), load_staged_rhs=slot)
                 slot = 1 - slot
                 yield
             for n in range(1 + slashes, listed, 2):
-                pltpu.matmul_push_rhs(weights[pair, n * BLK : (n + 2) * BLK, :], slot, m)
-                lhs = beside(*[listed_pair(v_buf, first + pair, n + u)[0] for u in range(2)])
+                both = [weights[pair, half, n * BLK : (n + 2) * BLK, :] for half in range(2)]
+                pltpu.matmul_push_rhs(beside(*both), slot, m)
+                lhs = beside(*[listed_pair(v_buf, head, i, n + u)[0] for u in range(2)])
                 pltpu.matmul_acc_lhs(acc, stacked(lhs, ones), load_staged_rhs=slot)
                 slot = 1 - slot
                 yield
@@ -514,20 +638,22 @@
                     pass
             for u in range(MIX_UNROLL):
                 for m in range(2):
-                    r, head, i = pair_of(first + at + 2 * u + m)
+                    head, _, i = pair_of(first + at + 2 * u + m)
                     mixed = pltpu.matmul_pop(accs[m * MIX_UNROLL + u])
                     for half in range(2):
                         out = mixed[:width, half_columns(half)] / mixed[width : width + 1, half_columns(half)]
                         rows = pl.ds(pl.multiple_of((i + half) * BLK, BLK), BLK)
                         staged[head, rows, :] = out.T.astype(jnp.bfloat16)
-            for u in range(2 * MIX_UNROLL // pairs_of_share):
-                r, head, i = pair_of(first + at + u * pairs_of_share)
-
-                @pl.when(r < groups - 1)
+            for u in range(2 * MIX_UNROLL):
+                head, q, _ = pair_of(first + at + u)
+                r = lax.div(q, pairs_of_share)
+                whole = lax.rem(q, pairs_of_share) == pairs_of_share - 1
+
+                @pl.when(whole & (r < groups - 1))
                 def _():
                     out_copy(head, r).start()
 
-                @pl.when(r == groups - 1)
+                @pl.when(whole & (r == groups - 1))
                 def _():
                     out_own(head).start()
 
@@ -554,9 +680,13 @@
             for c in range(PIECES):
                 if t < chain_len - 1:
 
-                    @pl.when((place >= t) & has_next)
+                    runs = chain_runs(t)
+                    if GATED and t < 2 and kv == 0:
+                        runs = runs & (second == 1)
+
+                    @pl.when(runs)
                     def _():
-                        chain(t, kv, c).wait_send()
+                        chain_of(t, kv, c).wait_send()
 
                 for sender in range(2):
                     runs = cross_runs(t, sender, sender)
@@ -609,26 +739,29 @@
         out_specs=anywhere,
         out_shape=jax.ShapeDtypeStruct((rows // groups, groups * heads * width), jnp.bfloat16),
         scratch_shapes=[
-            pltpu.SMEM((heads * blocks * slashes,), jnp.int32),
-            pltpu.SMEM((heads * blocks * slashes,), jnp.float32),
-            pltpu.SMEM((heads * blocks * verticals,), jnp.float32),
-            pltpu.SMEM((slabs * blocks,), jnp.int32),
-            pltpu.SMEM((slabs * blocks,), jnp.int32),
+            pltpu.SMEM(((slabs * blocks + 31) // 32,), jnp.int32),
+            pltpu.SMEM((heads,), jnp.int32),
             pltpu.SMEM((vertical.size,), jnp.int32),
             pltpu.SMEM((CAP,), jnp.int32),
+            pltpu.SMEM((CAP,), jnp.int32),
+            pltpu.SMEM((blocks // 2,), jnp.int32),
+            pltpu.SMEM((2 * listed,), jnp.float32),
+            pltpu.SMEM((2 * listed,), jnp.float32),
             pltpu.VMEM(queries.shape, jnp.bfloat16),
             pltpu.VMEM((slabs * (blocks + CAP), BLK, width), jnp.bfloat16),
             pltpu.VMEM((slabs * (blocks + CAP), width, BLK), jnp.bfloat16),
             pltpu.VMEM((heads, rows, width), jnp.bfloat16),
-            pltpu.VMEM((pairs // rounds, listed * BLK, 2 * BLK), jnp.bfloat16),
+            pltpu.VMEM((pairs // rounds, 2, listed * BLK, BLK), jnp.bfloat16),
             pltpu.VMEM((listed * BLK, 2 * BLK), jnp.float32),
             pltpu.VMEM((listed * BLK, 2 * BLK), jnp.float32),
             pltpu.VMEM((8, 2 * BLK), jnp.float32),
             pltpu.VMEM((8, 2 * BLK), jnp.float32),
             pltpu.VMEM((2, blocks, BLK, width), jnp.bfloat16),
             pltpu.VMEM((2, CAP, BLK, width), jnp.bfloat16),
+            pltpu.VMEM((2, CAP, BLK, width), jnp.bfloat16),
+            pltpu.SemaphoreType.REGULAR,
             dma((2,)),
-            dma((3,)),
+            dma((4,)),
             dma(hops),
             dma(hops),
             dma(hops),

time: 76.5 us -> 70.6 us (0.923)
  the two profiles are of different devices: /device:TPU:24 before, /device:TPU:17 now
where the time goes in v2:
time: 70.6 us; the launch traced here: 70.4 us
  Pallas kernels  67.2 us (95%)
  local copies, waits for them, and re-layouts  3.13 us (4%)
    pallas_call x1, Pallas kernels, shards(): pl.pallas_call(functools.partial(layer_kernel, blocks=blocks, rounds=roun...  67.2 us
    unnamed x1, local copies, waits for them, and re-layouts  3.13 us

profile of v2, /device:TPU:17, one launch (start us, length us, event | category | flops | bytes accessed | tf_op | source)
XLA Modules:
  0.0 70.4 jit_solution(6803716795935459713)
XLA Ops:
  0.0 67.2 %shard_map.55 = bf16[256,4096]{1,0:T(8,128)(2,1)} custom-call(s32[8,8]{1,0:T(8,128)} %slash_ref.1, s32[8,8]{1,0:T(8,128)} %vertical_ref.1, bf16[1024,1024]{1,0:T(8,128)(2,1)} %queries_ref.1, bf16[8,128,128]{2,1,0:T(8,128)(2,1)} %bitcast.2, bf16[8,128,128]{2,1,0:T(8,128)(2,1)} %bitcast.3), custom_call_target="tpu_custom_call" | custom-call | tf_op jit(solution)/shard_map/pallas_call | solution.py:728
  67.3 3.1 %copy.7 = bf16[256,4096]{1,0:T(8,128)(2,1)} copy(bf16[256,4096]{1,0:T(8,128)(2,1)} %shard_map.55) | data formatting | bytes 4194304

commit v3 on v2

--- a/solution.py
+++ b/solution.py
@@ -14,9 +14,10 @@
 CAP = 4
 NEG = -1e30
 PIECES = 2
-VALUE_STEPS = (3, 7, 8, 9, 12)
-MIX_UNROLL = 4
-GATED = True
+FIRST_STEPS = (1, 1, 3, 4)
+SECOND_STEPS = (3, 7)
+MIX_UNROLL = 2
+ROUNDS = 2
 RING = 8
 VMEM_BYTES = 62 * 1024 * 1024
 SPARE_BYTES = 3 * 1024 * 1024
@@ -326,12 +327,9 @@
     second = group % 2
     partner = group + 1 - 2 * second
     loads[0].wait()
-
-    @pl.when(second == 0)
-    def _():
-        for c in range(PIECES):
-            start_chain(0, 0, c)
-            start_cross(0, 0, c, False)
+    for c in range(PIECES):
+        start_chain(0, 0, c)
+        start_cross(0, 0, c, False)
 
     words = tuple(jnp.int32(0) for _ in range((whole_blocks + 31) // 32))
     for w, word in enumerate(lax.fori_loop(0, heads, names, words)):
@@ -340,38 +338,38 @@
     loads[3].wait()
     loads[1].wait()
 
-    @pl.when(second == 1)
-    def _():
-        if GATED:
-            pl.semaphore_wait(turn_sem, 1)
-        for c in range(PIECES):
-            start_chain(0, 0, c)
-            start_cross(0, 0, c, False)
-
     start_direct(0)
     list_pack(pack_ref, jnp.maximum((place - pack_at) * 2 + side, 0))
     for t in order:
         for c in range(PIECES):
             pass_on(t, 0, c)
         if t == 1:
-            if GATED:
-
-                @pl.when(second == 0)
-                def _():
-                    for sent_t in range(min(2, chain_len - 1)):
-                        for c in range(PIECES):
-
-                            @pl.when(chain_runs(sent_t))
-                            def _():
-                                chain_of(sent_t, 0, c).wait_send()
-
-                    pl.semaphore_signal(
-                        turn_sem, 1, device_id={"head": partner}, device_id_type=MESH
-                    )
-
             lax.fori_loop(0, heads, place_verticals, 0)
             for n in range(blocks):
                 v_buf[own_first + n] = held[1, n].T
+    def send_values():
+        for c in range(PIECES):
+            start_chain(0, 1, c)
+            start_cross(0, 1, c, False)
+        start_direct(1)
+
+    early_sent = min(2, chain_len - 1)
+
+    def give_turn():
+        for t in range(early_sent):
+            for c in range(PIECES):
+
+                @pl.when(chain_runs(t))
+                def _():
+                    chain_of(t, 1, c).wait_send()
+
+        pl.semaphore_signal(turn_sem, 1, device_id={"head": partner}, device_id_type=MESH)
+
+    def take_turn():
+        pl.semaphore_wait(turn_sem, 1)
+        send_values()
+
+    pl.when(second == 0)(send_values)
     wait_cross(0)
     loads[2].wait()
 
@@ -420,10 +418,19 @@
     pairs = heads * blocks // 2 // rounds
     pairs_of_share = share // 2
     chunk_count = slashes // 2 + 1
-    values_due = [[(0, c) for c in range(PIECES)]]
-    for t in order:
-        each = [[(t, c)] for c in range(PIECES)]
-        values_due += [sum(each, [])] if t >= pack_at else each
+    def relays(ts):
+        return [functools.partial(pass_on, t, 1, c) for t in ts for c in range(PIECES)]
+
+    first_relays = relays(order[:1])
+    later_relays = relays(order[1:-1])
+    last_relays = relays(order[-1:])
+    if len(order) < 2:
+        later_relays, last_relays = [], []
+    events = [(FIRST_STEPS[0], 0, first_relays[:1]), (FIRST_STEPS[1], 0, first_relays[1:])]
+    events += [(FIRST_STEPS[2], 0, [give_turn, *later_relays])]
+    events += [(FIRST_STEPS[3], 0, last_relays)]
+    events += [(SECOND_STEPS[0], 1, [take_turn])]
+    events += [(SECOND_STEPS[1], 1, first_relays + later_relays + last_relays)]
 
     for q in range(blocks // 2):
         block_ref[q] = owner_of(q // pairs_of_share) * share + q % pairs_of_share * 2
@@ -581,18 +588,12 @@
 
         def two_pairs(step, carry):
             if first == 0:
-                for k, due in enumerate(values_due):
-
-                    @pl.when(step == min(VALUE_STEPS[min(k, len(VALUE_STEPS) - 1)], pairs // 2 - 1))
+                for at, of, acts in events:
+
+                    @pl.when((step == min(at, pairs // 2 - 1)) & (second == of))
                     def _():
-                        for t, c in due:
-                            if t == 0:
-                                start_cross(0, 1, c, False)
-                                start_chain(0, 1, c)
-                            else:
-                                pass_on(t, 1, c)
-                        if k == 0:
-                            start_direct(1)
+                        for act in acts:
+                            act()
 
             carry = one_pair(2 * step, 0, *carry)
             return one_pair(2 * step + 1, 1, *carry)
@@ -681,7 +682,7 @@
                 if t < chain_len - 1:
 
                     runs = chain_runs(t)
-                    if GATED and t < 2 and kv == 0:
+                    if kv == 1 and t < early_sent:
                         runs = runs & (second == 1)
 
                     @pl.when(runs)
@@ -719,7 +720,7 @@
     pairs = heads * blocks // 2
     room = VMEM_BYTES - 4 * (2 * BLK * width * slabs * (blocks + CAP) // 2)
     room -= 4 * rows * heads * width + 2 * 4 * listed * BLK * 2 * BLK + SPARE_BYTES
-    rounds = 1
+    rounds = ROUNDS
     while pairs // rounds * listed * BLK * 2 * BLK * 2 > room:
         rounds *= 2
     dma = pltpu.SemaphoreType.DMA

time: 70.6 us -> 66.8 us (0.946)
  the two profiles are of different devices: /device:TPU:17 before, /device:TPU:25 now
where the time goes in v3:
time: 66.8 us; the launch traced here: 66.4 us
  Pallas kernels  63.2 us (95%)
  local copies, waits for them, and re-layouts  3.13 us (5%)
    pallas_call x1, Pallas kernels, shards(): pl.pallas_call(functools.partial(layer_kernel, blocks=blocks, rounds=roun...  63.2 us
    unnamed x1, local copies, waits for them, and re-layouts  3.13 us

profile of v3, /device:TPU:25, one launch (start us, length us, event | category | flops | bytes accessed | tf_op | source)
XLA Modules:
  0.0 66.4 jit_solution(2392309945400582043)
XLA Ops:
  0.0 63.2 %shard_map.55 = bf16[256,4096]{1,0:T(8,128)(2,1)} custom-call(s32[8,8]{1,0:T(8,128)} %slash_ref.1, s32[8,8]{1,0:T(8,128)} %vertical_ref.1, bf16[1024,1024]{1,0:T(8,128)(2,1)} %queries_ref.1, bf16[8,128,128]{2,1,0:T(8,128)(2,1)} %bitcast.2, bf16[8,128,128]{2,1,0:T(8,128)(2,1)} %bitcast.3), custom_call_target="tpu_custom_call" | custom-call | tf_op jit(solution)/shard_map/pallas_call | solution.py:729
  63.2 3.1 %copy.7 = bf16[256,4096]{1,0:T(8,128)(2,1)} copy(bf16[256,4096]{1,0:T(8,128)(2,1)} %shard_map.55) | data formatting | bytes 4194304
